TPU v7x, 256 devices: a whole 4x4x8 slice. The times are simulated.
256 devices in a mesh: dp: 4 (over x), seq: 64 (over y, z, core).
Axes of the slice: x: 4, y: 4, z: 8, core: 2. Of those that a mesh axis runs over, the one named last changes fastest.
Arguments:
- tiles: bfloat16 [4, 65536, 768], P('dp', 'seq'), may hold values from -48 to 48
- tile_count: int32 [4], P('dp'), may hold values from 32769 to 65536
- offsets: int32 [16], replicated, may hold values from 0 to 15
- w_query: bfloat16 [768, 768], replicated, may hold values from -0.375 to 0.375
- w_key: bfloat16 [768, 768], replicated, may hold values from -0.375 to 0.375
- w_value: bfloat16 [768, 768], replicated, may hold values from -0.21875 to 0.21875
- w_out: bfloat16 [768, 768], replicated, may hold values from -0.21875 to 0.21875
- cotangent: bfloat16 [4, 65536, 768], P('dp', 'seq'), may hold values from -0.03125 to 0.03125
Outputs:
- branch: bfloat16 [4, 65536, 768], P('dp', 'seq')
- grad_out: float32 [768, 768], P(None, 'seq')
All inputs are finite; a program needn't handle non-finite values.
Results may differ from a plain program's by a relative error of at most 0.0095.
The roundings to bfloat16 on the way count: a program that leaves them out, or rounds other values in their place, can miss the bound.
Values may be sent and summed in bfloat16 or wider, within the bound.
No kernel may reach another device: no remote copies, remote signals or barrier semaphores. Data moves between devices by JAX's collectives and lax.ppermute only.
A program may use at most 128 MiB of HBM per device.

v0:
```python
import functools

import jax
import jax.numpy as jnp
from jax import lax
from jax.experimental import pallas as pl
from jax.experimental.pallas import tpu as pltpu
from jax.sharding import PartitionSpec as P


D = 768
HEADS = 16
HEAD = 48
SEG = 1024
RATE = 16
PICKED = SEG // RATE
PAIRS = HEADS // 2
SHARDS = 64
EARLY = 3
FLOOR = -1e30
LOCAL_VMEM = 28 << 20
BRANCH_VMEM = 16 << 20
LOG2E = 1.4426950408889634
SCALE2 = HEAD ** (-0.5) * LOG2E

f32 = jnp.float32
bf16 = jnp.bfloat16


def lanes(shape):
    return lax.broadcasted_iota(jnp.int32, shape, len(shape) - 1)


def rows(shape):
    return lax.broadcasted_iota(jnp.int32, shape, len(shape) - 2)


def hbm(a):
    return pltpu.with_memory_space_constraint(a, pltpu.HBM)


def vmem(a):
    return pltpu.with_memory_space_constraint(a, pltpu.VMEM)


def nt(a, b):
    return lax.dot_general(a, b, (((1,), (1,)), ((), ())), preferred_element_type=f32)


def nn(a, b):
    return jnp.dot(a, b, preferred_element_type=f32)


HBM = pl.BlockSpec(memory_space=pltpu.HBM)
SMEM = pl.BlockSpec(memory_space=pltpu.SMEM)
VMEM = pl.BlockSpec(memory_space=pltpu.VMEM)


def pick_kernel(off_ref, x_hbm, wq_hbm, wk_hbm, wv_hbm, send_ref, x_ref, w_ref, x2_ref, sems):
    copies = []
    for b in range(4):
        r = pl.ds(256 * b, 256)
        copies.append(pltpu.make_async_copy(x_hbm.at[r], x_ref.at[r], sems.at[b]))
    for n, hbm in enumerate((wq_hbm, wk_hbm, wv_hbm)):
        for t in range(3):
            r = pl.ds(256 * t, 256)
            copies.append(pltpu.make_async_copy(hbm.at[:, r], w_ref.at[n, :, r], sems.at[4 + 3 * n + t]))
    for copy in copies:
        copy.start()
    c = lanes((16, 256))
    same = c // 16 == rows((16, 256))
    onehot = jnp.concatenate([(same & (c % 16 == off_ref[h])).astype(f32) for h in range(HEADS)], axis=0).astype(bf16)
    for b in range(4):
        copies[b].wait()
        y = nn(onehot, x_ref[b * 256 : (b + 1) * 256, :]).astype(bf16)
        for h in range(HEADS):
            x2_ref[h * 64 + b * 16 : h * 64 + b * 16 + 16, :] = y[h * 16 : (h + 1) * 16, :]
    sel = []
    col = lanes((64, 256))
    for n in range(3):
        parts = []
        for t in range(3):
            copies[4 + 3 * n + t].wait()
            y = nn(x2_ref[320 * t : 320 * t + 384, :], w_ref[n, :, 256 * t : 256 * t + 256])
            out = y[0:64]
            for k in range(1, 6):
                start = (5 * t + k) * HEAD - 256 * t
                out = jnp.where(col >= start, y[64 * k : 64 * k + 64], out)
            parts.append(out)
        sel.append(jnp.concatenate(parts, axis=1))
    q, k, v = sel
    lane = lanes((64, 128))
    for h in range(HEADS):
        t = min(48 * h // 128, 4)
        o = 48 * h - 128 * t

        def moved(a, to):
            return pltpu.roll(a[:, 128 * t : 128 * t + 256], (to - o) % 256, 1)[:, :128]

        kv = jnp.where(lane < 48, moved(k, 0), moved(v, 48))
        q_low = moved(q, 96)
        q_high = moved(q, 64)
        for j in range(4):
            s = slice(16 * j, 16 * j + 16)
            mine = jnp.concatenate([q_low[s], q_high[s], q_low[0:32]], axis=0)
            send_ref[4 * h + j] = jnp.where(lane < 96, kv, mine).astype(bf16)


def pick(offsets, x, wq, wk, wv):
    return pl.pallas_call(
        pick_kernel,
        in_specs=[SMEM, HBM, HBM, HBM, HBM],
        out_shape=[
            jax.ShapeDtypeStruct((SHARDS, PICKED, 128), bf16),
            pltpu.VMEM((SEG, D), bf16),
        ],
        out_specs=[VMEM, VMEM],
        scratch_shapes=[
            pltpu.VMEM((3, D, D), bf16),
            pltpu.VMEM((SEG, D), bf16),
            pltpu.SemaphoreType.DMA((13,)),
        ],
        compiler_params=pltpu.CompilerParams(vmem_limit_bytes=24 << 20),
        name="pick",
    )(hbm(offsets), hbm(x), hbm(wq), hbm(wk), hbm(wv))


def local_kernel(first, groups, rank_ref, count_ref, off_ref, x_ref, wq_hbm, wk_hbm, wv_hbm, *refs):
    step = pl.program_id(0)
    if first == 0:
        cot_hbm, attn_ref, so_ref, sl_ref, out_hbm, w_ref, o_s, l_s, cot_s, out_s, sems = refs
        load = pltpu.make_async_copy(cot_hbm, cot_s, sems.at[18])
        store = pltpu.make_async_copy(out_s, out_hbm, sems.at[19])
    else:
        attn_ref, so_ref, sl_ref, w_ref, o_s, l_s, sems = refs
    tiles = {g: [3 * g // 2, 3 * g // 2 + 1] for g in range(first, first + groups)}
    windows = {}
    for g, new in tiles.items():
        for u in new:
            if u not in windows:
                r = pl.ds(128 * u, 128)
                windows[u] = (g - first, [
                    pltpu.make_async_copy(hbm.at[:, r], w_ref.at[n, :, r], sems.at[3 * u + n])
                    for n, hbm in enumerate((wq_hbm, wk_hbm, wv_hbm))
                ])

    @pl.when(step == 0)
    def _():
        for _, copies in windows.values():
            for copy in copies:
                copy.start()
        if first == 0:
            load.start()

    for at, copies in windows.values():

        @pl.when(step == at)
        def _(copies=copies):
            for copy in copies:
                copy.wait()

    here = 2 * step
    g = step + first
    t = (3 * g) // 2
    shift = 192 * g - 128 * t
    wl = lanes((D, 128))
    weights = []
    for part in range(2):
        for n in range(3):
            w = w_ref[n, :, pl.ds(pl.multiple_of(128 * t, 128), 256)].astype(f32)
            w = pltpu.roll(w, 256 - 96 * part - shift, 1)[:, :128]
            weights.append(jnp.where(wl < 96, w, 0.0).astype(bf16))
    qkv = nn(x_ref[...], jnp.concatenate(weights, axis=1))
    lane = lanes((SEG, 128))
    live = rows((SEG, 128)) + rank_ref[0] * SEG < count_ref[0]
    bias = jnp.where(live, 0.0, FLOOR)
    ones = jnp.ones((SEG, 128), f32)
    bl = lanes((256, 128))
    sel = lanes((PICKED, 128)) < 48
    for part in range(2):
        qf, kf, vf = (qkv[:, 384 * part + 128 * n : 384 * part + 128 * n + 128] for n in range(3))
        q = jnp.where(lane == 96, 1.0, qf).astype(bf16)
        kf = jnp.where(lane == 96, bias, kf)
        v = jnp.concatenate([vf, ones], axis=1).astype(bf16)
        inside = (lane < 48, (lane >= 48) & (lane < 96))
        kh = [jnp.where(i | (lane == 96), kf, 0.0).astype(bf16) for i in inside]
        for b in range(4):
            r = slice(256 * b, 256 * b + 256)
            both = []
            for a in range(2):
                s = nt(q[r], kh[a])
                m = jnp.max(s, axis=1, keepdims=True)
                e = jnp.exp2((s - m) * SCALE2).astype(bf16)
                o = nn(e, v)
                total = o[:, 128:256]
                both.append((o[:, 0:128] / total, m * SCALE2 + jnp.log2(total)))
            out = jnp.where(bl < 48, both[0][0], both[1][0])
            attn_ref[part, r, :] = out.astype(bf16)
            o_s[part, r, :] = out
            l_s[part, r, :] = jnp.where(bl < 48, both[0][1], both[1][1])
        even = pl.ds(off_ref[4 * g + 2 * part], PICKED, stride=RATE)
        odd = pl.ds(off_ref[4 * g + 2 * part + 1], PICKED, stride=RATE)
        so_ref[here + part] = jnp.where(sel, o_s[part, even, :], o_s[part, odd, :])
        sl_ref[here + part] = jnp.where(sel, l_s[part, even, :], l_s[part, odd, :])


    if first == 0:

        @pl.when(step == 1)
        def _():
            load.wait()
            reorder_cotangent(rank_ref[0], cot_s, out_s)
            store.start()

        @pl.when(step == groups - 1)
        def _():
            store.wait()


def reorder_cotangent(rank, cot_ref, out_ref):
    y, c = rank // 16, rank % 2
    n = rows((96, D))
    offset = lanes((96, D)) - n - 12 * ((n * 171) // 2048)

    def half(i, carry):
        blocks = []
        for k in range(4):
            owner = ((y + k) % 4) * 16 + (c + i) % 2
            blocks.append((offset == 12 * owner).astype(f32))
        onehot = jnp.concatenate(blocks, axis=0).astype(bf16)
        out_ref[pl.ds(pl.multiple_of(384 * i, 384), 384), :] = nt(onehot, cot_ref[...]).astype(bf16)
        return carry

    lax.fori_loop(0, 2, half, 0)


def local(first, groups, rank, count, offsets, x, weights, cot=None):
    out_specs = [pl.BlockSpec((2, SEG, 128), lambda p: (p, 0, 0)), VMEM, VMEM]
    out_shape = [
        pltpu.HBM((2 * groups, SEG, 128), bf16),
        pltpu.VMEM((2 * groups, PICKED, 128), f32),
        pltpu.VMEM((2 * groups, PICKED, 128), f32),
    ]
    scratch = [pltpu.VMEM((3, D, D), bf16), pltpu.VMEM((2, SEG, 128), f32), pltpu.VMEM((2, SEG, 128), f32)]
    operands = (rank, count, offsets, vmem(x), *(hbm(w) for w in weights))
    in_specs = [SMEM, SMEM, SMEM, VMEM, HBM, HBM, HBM]
    if first == 0:
        out_specs.append(HBM)
        out_shape.append(pltpu.HBM((D, SEG), bf16))
        scratch += [pltpu.VMEM((SEG, D), bf16), pltpu.VMEM((D, SEG), bf16)]
        operands += (hbm(cot),)
        in_specs.append(HBM)
    scratch.append(pltpu.SemaphoreType.DMA((20,)))
    return pl.pallas_call(
        functools.partial(local_kernel, first, groups),
        grid=(groups,),
        in_specs=in_specs,
        out_specs=out_specs,
        out_shape=out_shape,
        scratch_shapes=scratch,
        compiler_params=pltpu.CompilerParams(
            dimension_semantics=("arbitrary",), vmem_limit_bytes=LOCAL_VMEM
        ),
        cost_estimate=pl.CostEstimate(flops=6_000_000_000 * groups, transcendentals=groups << 22, bytes_accessed=8 << 20),
        name="local",
    )(*operands)


def far_kernel(rank_ref, count_ref, off_ref, recv_ref, ret_ref, after_ref, kb_s, v_s, q_s):
    after_ref[0] = count_ref[0]
    kv = recv_ref[...].reshape(SHARDS * PICKED, 128).astype(f32)
    lane = lanes(kv.shape)
    live = rows(kv.shape) * RATE + off_ref[rank_ref[0] // 4] < count_ref[0]
    kb_s[...] = jnp.where(lane == 112, jnp.where(live, 0.0, FLOOR), kv).astype(bf16)
    v_s[:, 0:128] = kv.astype(bf16)
    v_s[:, 128:256] = jnp.ones(kv.shape, bf16)
    low = recv_ref[:, 0:16, :].reshape(SEG, 128).astype(f32)
    high = recv_ref[:, 16:32, :].reshape(SEG, 128).astype(f32)
    ql = lanes((SEG, 128))
    q = jnp.where(ql < 32, pltpu.roll(low, 32, 1), pltpu.roll(high, 64, 1))
    q_s[...] = jnp.where(ql < 48, q, jnp.where(ql == 112, 1.0, 0.0)).astype(bf16)
    bl = lanes((256, 128))
    hl = lanes((16, 8, 128))
    for b in range(4):
        s = nt(q_s[256 * b : 256 * b + 256, :], kb_s[...])
        m = jnp.max(s, axis=1, keepdims=True)
        e = jnp.exp2((s - m) * SCALE2).astype(bf16)
        o = nn(e, v_s[...])
        total = o[:, 128:256]
        out = pltpu.roll(o[:, 0:128] / total, 80, 1)
        level = m * SCALE2 + jnp.log2(total)
        part0 = level.astype(bf16).astype(f32)
        part1 = (level - part0).astype(bf16).astype(f32)
        part2 = level - part0 - part1
        out = jnp.where(bl < 48, out, jnp.where(bl == 48, part0, jnp.where(bl == 49, part1, part2)))
        out = out.reshape(16, 16, 128)
        second = pltpu.roll(out[:, 8:16, :], 64, 2)
        ret_ref[16 * b : 16 * b + 16] = jnp.where(hl < 64, out[:, 0:8, :], second).astype(bf16)


def far(rank, count, offsets, recv):
    return pl.pallas_call(
        far_kernel,
        in_specs=[SMEM, SMEM, SMEM, VMEM],
        out_specs=[VMEM, SMEM],
        out_shape=[jax.ShapeDtypeStruct((SHARDS, 8, 128), bf16), jax.ShapeDtypeStruct((1,), jnp.int32)],
        scratch_shapes=[
            pltpu.VMEM((SHARDS * PICKED, 128), bf16),
            pltpu.VMEM((SHARDS * PICKED, 256), bf16),
            pltpu.VMEM((SEG, 128), bf16),
        ],
        compiler_params=pltpu.CompilerParams(vmem_limit_bytes=32 << 20),
        cost_estimate=pl.CostEstimate(flops=6_000_000_000, transcendentals=4 << 20, bytes_accessed=2 << 20),
        name="far",
    )(rank, count, offsets, recv)


def natural(pair, n):
    lane = lanes((n, 128))
    out = []
    for t in range(6):
        p = 128 * t // 96
        o = 128 * t - 96 * p
        n0 = 96 - o
        a = pair(p)
        a = pltpu.roll(a, 128 - o, 1) if o else a
        out.append(jnp.where(lane < n0, a, pltpu.roll(pair(p + 1), n0, 1)))
    return jnp.concatenate(out, axis=1)


def merge_kernel(split, rank_ref, count_ref, off_ref, attn0_hbm, attn1_hbm, so0_ref, so1_ref, sl0_ref, sl1_ref, ret_ref, cot_hbm, attn_hbm, grad_ref, near_s, cot_s, attn_s, sems):
    loads = []
    for b in range(4):
        part = pl.ds(256 * b, 256)
        loads.append([
            pltpu.make_async_copy(attn0_hbm.at[:, part], near_s.at[0:split, part], sems.at[6 + 2 * b]),
            pltpu.make_async_copy(attn1_hbm.at[:, part], near_s.at[split:PAIRS, part], sems.at[7 + 2 * b]),
        ])
    last_load = pltpu.make_async_copy(cot_hbm, cot_s, sems.at[5])
    for copy in (*loads[0], *loads[1], *loads[2], *loads[3], last_load):
        copy.start()
    either = lambda early, late, p: early.at[p] if p < split else late.at[p - split]
    lane = lanes((PICKED, 128))
    merged = []
    for p in range(PAIRS):
        tiles, levels = [], []
        for h in (2 * p, 2 * p + 1):
            pieces = []
            for j in range(4):
                block = ret_ref[4 * h + j].astype(f32)
                pieces += [block, pltpu.roll(block, 64, 1)]
            tile = jnp.concatenate(pieces, axis=0)
            tiles.append(tile)
            levels.append(tile[:, 48:49] + tile[:, 49:50] + tile[:, 50:51])
        value = jnp.where(lane < 48, tiles[0], pltpu.roll(tiles[1], 48, 1))
        gap = jnp.where(lane < 48, levels[0], levels[1]) - either(sl0_ref, sl1_ref, p)[...]
        near = 1.0 / (1.0 + jnp.exp2(gap))
        distant = 1.0 / (1.0 + jnp.exp2(-gap))
        merged.append(near * either(so0_ref, so1_ref, p)[...] + distant * value)
    sel = natural(lambda p: merged[p], PICKED).astype(bf16)
    col = lanes((8, D))
    offcol = jnp.zeros((8, D), jnp.int32)
    for h in range(HEADS):
        offcol = jnp.where(col >= HEAD * h, off_ref[h], offcol)
    offcol = offcol[0:1]
    stores = []
    for b in range(4):
        r = slice(256 * b, 256 * b + 256)
        spread = (rows((256, PICKED)) // RATE + 16 * b == lanes((256, PICKED))).astype(bf16)
        far_rows = nn(spread, sel)
        for copy in loads[b]:
            copy.wait()
        near_rows = natural(lambda p: near_s[p, r, :].astype(f32), 256)
        row = rows((256, D))
        attn = jnp.where(row % RATE == offcol, far_rows, near_rows)
        attn = jnp.where(row + (rank_ref[0] * SEG + 256 * b) < count_ref[0], attn, 0.0).astype(bf16)
        attn_s[r, :] = attn
        part = pl.ds(256 * b, 256)
        stores.append(pltpu.make_async_copy(attn_s.at[part], attn_hbm.at[part], sems.at[b]))
        stores[b].start()
    last_load.wait()

    def half(i, carry):
        part = pl.ds(pl.multiple_of(384 * i, 384), 384)
        grad_ref[part, :] = nn(cot_s[part, :], attn_s[...]).astype(bf16)
        return carry

    lax.fori_loop(0, 2, half, 0)
    for store in stores:
        store.wait()


def merge(rank, count, offsets, near0, near1, ret, cot):
    split = near0[0].shape[0]
    return pl.pallas_call(
        functools.partial(merge_kernel, split),
        in_specs=[SMEM] * 3 + [HBM] * 2 + [VMEM] * 5 + [HBM],
        out_specs=[HBM, VMEM],
        out_shape=[pltpu.HBM((SEG, D), bf16), jax.ShapeDtypeStruct((D, D), bf16)],
        scratch_shapes=[
            pltpu.VMEM((PAIRS, SEG, 128), bf16),
            pltpu.VMEM((D, SEG), bf16),
            pltpu.VMEM((SEG, D), bf16),
            pltpu.SemaphoreType.DMA((14,)),
        ],
        compiler_params=pltpu.CompilerParams(vmem_limit_bytes=20 << 20),
        cost_estimate=pl.CostEstimate(flops=4_000_000_000, transcendentals=0, bytes_accessed=8 << 20),
        name="merge",
    )(rank, count, offsets, hbm(near0[0]), hbm(near1[0]), *(vmem(a) for n in (1, 2) for a in (near0[n], near1[n])), vmem(ret), hbm(cot))


def branch_kernel(attn_ref, wout_ref, branch_ref):
    branch_ref[...] = nn(attn_ref[...], wout_ref[...]).astype(bf16)


def project_out(attn, wout):
    rows_of = pl.BlockSpec((256, D), lambda b: (b, 0))
    return pl.pallas_call(
        branch_kernel,
        grid=(4,),
        in_specs=[rows_of, pl.BlockSpec((D, D), lambda b: (0, 0))],
        out_specs=rows_of,
        out_shape=jax.ShapeDtypeStruct((SEG, D), bf16),
        compiler_params=pltpu.CompilerParams(dimension_semantics=("arbitrary",), vmem_limit_bytes=BRANCH_VMEM),
        cost_estimate=pl.CostEstimate(flops=1_300_000_000, transcendentals=0, bytes_accessed=5 << 20),
        name="branch",
    )(hbm(attn), hbm(wout))


def place(y, z, c):
    return (y * 8 + z) * 2 + c


EVERY = [(y, z, c) for y in range(4) for z in range(8) for c in range(2)]
Z_GROUPS = [[place(y, z, c) for z in range(8)] for y in range(4) for c in range(2)]


def to_partner(a):
    return lax.ppermute(a, "seq", [(place(y, z, c), place(y, z, 1 - c)) for y, z, c in EVERY])


def along_y(a, k):
    return lax.ppermute(a, "seq", [(place(y, z, c), place((y + k) % 4, z, c)) for y, z, c in EVERY])


def across_slides(a, k):
    return lax.ppermute(a, "dp", [(x, x ^ k) for x in range(4)])


def reduce_gradient(grad):
    got = to_partner(grad[D // 2 :])
    half = (grad[: D // 2].astype(f32) + got.astype(f32)).astype(bf16)
    blocks = [half[96 * k : 96 * k + 96] for k in (1, 2, 3)]
    got = [along_y(blocks[k - 1], k) for k in (1, 2, 3)]
    part = half[:96].astype(f32) + got[0].astype(f32) + (got[1].astype(f32) + got[2].astype(f32))
    blocks = part.astype(bf16).reshape(8, 12, D)
    blocks = lax.all_to_all(blocks, "seq", 0, 0, tiled=True, axis_index_groups=Z_GROUPS)
    mine = blocks.astype(f32).sum(axis=0)
    got = [across_slides(mine, k) for k in (1, 2, 3)]
    return ((mine + got[0]) + (got[1] + got[2])).T


def body(tiles, tile_count, offsets, w_query, w_key, w_value, w_out, cotangent):
    x = tiles[0]
    rank = lax.axis_index("seq")
    rank = rank.astype(jnp.int32)[None]
    weights = (w_query, w_key, w_value)
    send, x = pick(offsets, x, *weights)
    recv = lax.all_to_all(send, "seq", 0, 0, tiled=True)
    *near0, cot = local(0, EARLY, rank, tile_count, offsets, x, weights, cotangent[0])
    ret, after = far(rank, tile_count, offsets, recv)
    back = lax.all_to_all(ret, "seq", 0, 0, tiled=True)
    near1 = local(EARLY, 4 - EARLY, rank, after, offsets, x, weights)
    attn, grad = merge(rank, tile_count, offsets, near0, near1, back, cot)
    branch = project_out(attn, w_out)
    return branch[None], reduce_gradient(grad)


def solution(mesh):
    in_specs = (P("dp", "seq", None), P("dp"), P(), P(), P(), P(), P(), P("dp", "seq", None))
    out_specs = (P("dp", "seq", None), P(None, "seq"))
    return jax.shard_map(body, mesh=mesh, in_specs=in_specs, out_specs=out_specs, check_vma=False)
```

profile of v0, /device:TPU:6, one launch (start us, length us, event | category | flops | bytes accessed | tf_op | source)
XLA Modules:
  0.0 121.5 jit_solution(18405293084090341062)
XLA Ops:
  0.6 8.0 %pick.1 = (bf16[64,64,128]{2,1,0:T(8,128)(2,1)}, bf16[1024,768]{1,0:T(8,128)(2,1)S(1)}) custom-call(s32[16]{0:T(128)} %off_ref.9, bf16[1024,768]{1,0:T(8,128)(2,1)} %bitcast.6, bf16[768,768]{1,0:T(8,128)(2,1)} %wq_hbm.5, bf16[768,768]{1,0:T(8,128)(2,1)} %wk_hbm.5, bf16[768,768]{1,0:T(8,128)(2,1)} %wv_hbm.5), custom_call_target="tpu_custom_call" | custom-call | tf_op jit(solution)/shard_map/pick/pallas_call | solution.py:110
  8.6 0.0 copy-start
  8.7 12.1 %all-to-all-start = ((bf16[64,64,128]{2,1,0:T(8,128)(2,1)}), bf16[64,64,128]{2,1,0:T(8,128)(2,1)S(1)}, u32[]{:S(2)}, u32[]{:S(2)}) async-start(bf16[64,64,128]{2,1,0:T(8,128)(2,1)} %get-tuple-element.17), calls=%async_computation | async-start | bytes 2097152 | tf_op jit(solution)/shard_map/all_to_all | solution.py:469
  21.4 0.0 copy-done
  21.4 25.6 %local.2 = (bf16[6,1024,128]{2,1,0:T(8,128)(2,1)}, f32[6,64,128]{2,1,0:T(8,128)S(1)}, f32[6,64,128]{2,1,0:T(8,128)S(1)}, bf16[768,1024]{1,0:T(8,128)(2,1)}) custom-call(s32[1]{0:T(128)} %bitcast.rank_ref, s32[1]{0:T(128)S(6)} %copy.10.count_ref, s32[16]{0:T(128)S(1)} %copy-done, bf16[1024,768]{1,0:T(8,128)(2,1)S(1)} %get-tuple-element.15.x_ref, ...), custom_call_target="tpu_custom_call" | custom-call | flops 17999998976 | bytes 8388608 | tf_op jit(solution)/shard_map/local/pallas_call | solution.py:254
  47.1 1.8 %all-to-all-done.recv_ref = bf16[64,64,128]{2,1,0:T(8,128)(2,1)S(1)} async-done(((bf16[64,64,128]{2,1,0:T(8,128)(2,1)}), bf16[64,64,128]{2,1,0:T(8,128)(2,1)S(1)}, u32[]{:S(2)}, u32[]{:S(2)}) %all-to-all-start) | async-done | bytes 1048608 | tf_op jit(solution)/shard_map/all_to_all | solution.py:469
  48.9 7.7 %far.1 = (bf16[64,8,128]{2,1,0:T(8,128)(2,1)}, s32[1]{0:T(128)}) custom-call(s32[1]{0:T(128)} %bitcast.rank_ref, s32[1]{0:T(128)S(6)} %copy.10.count_ref, s32[16]{0:T(128)S(1)} %copy-done, bf16[64,64,128]{2,1,0:T(8,128)(2,1)S(1)} %all-to-all-done.recv_ref), custom_call_target="tpu_custom_call" | custom-call | flops 6000000000 | bytes 2097152 | tf_op jit(solution)/shard_map/far/pallas_call | solution.py:302
  56.6 8.7 %all-to-all-start.1 = ((bf16[64,8,128]{2,1,0:T(8,128)(2,1)}), bf16[64,8,128]{2,1,0:T(8,128)(2,1)S(1)}, u32[]{:S(2)}, u32[]{:S(2)}) async-start(bf16[64,8,128]{2,1,0:T(8,128)(2,1)} %get-tuple-element.24), calls=%async_computation.1 | async-start | bytes 262144 | tf_op jit(solution)/shard_map/all_to_all | solution.py:472
  65.3 10.4 %local.3 = (bf16[2,1024,128]{2,1,0:T(8,128)(2,1)}, f32[2,64,128]{2,1,0:T(8,128)S(1)}, f32[2,64,128]{2,1,0:T(8,128)S(1)}) custom-call(s32[1]{0:T(128)} %bitcast.rank_ref, s32[1]{0:T(128)} %get-tuple-element.18.count_ref, s32[16]{0:T(128)S(1)} %copy-done, bf16[1024,768]{1,0:T(8,128)(2,1)S(1)} %get-tuple-element.15.x_ref, bf16[768,768]{1,0:T(8,128)(2,1)} %wq_hbm.5, ...), custom_call_target="tpu_custom_call" | custom-call | flops 6000000000 | bytes 8388608 | tf_op jit(solution)/shard_map/local/pallas_call | solution.py:254
  75.7 0.0 all-to-all-done.1.ret_ref
  75.7 5.8 %merge.1 = (bf16[1024,768]{1,0:T(8,128)(2,1)}, bf16[768,768]{1,0:T(8,128)(2,1)S(1)}) custom-call(s32[1]{0:T(128)} %bitcast.rank_ref, s32[1]{0:T(128)S(6)} %copy.10.count_ref, s32[16]{0:T(128)S(1)} %copy-done, bf16[6,1024,128]{2,1,0:T(8,128)(2,1)} %get-tuple-element.16.attn0_hbm, bf16[2,1024,128]{2,1,0:T(8,128)(2,1)} %get-tuple-element.19.attn1_hbm, ...), custom_call_target="tpu_custom_call" | custom-call | flops 4000000000 | bytes 8388608 | tf_op jit(solution)/shard_map/merge/pallas_call | solution.py:395
  81.6 0.1 collective-permute-start
  81.7 2.0 %collective-permute-done = bf16[384,768]{1,0:T(8,128)(2,1)S(1)} collective-permute-done((bf16[384,768]{1,0:T(8,128)(2,1)S(1)}, bf16[384,768]{1,0:T(8,128)(2,1)S(1)}, u32[]{:S(2)}, u32[]{:S(2)}) %collective-permute-start) | collective-permute-done | bytes 589856 | tf_op jit(solution)/shard_map/ppermute | solution.py:439
  83.7 0.2 add_convert_fusion
  83.9 1.4 %collective-permute-start.1 = (bf16[96,768]{1,0:T(8,128)(2,1)S(1)}, bf16[96,768]{1,0:T(8,128)(2,1)S(1)}, u32[]{:S(2)}, u32[]{:S(2)}) collective-permute-start(bf16[96,768]{1,0:T(8,128)(2,1)S(1)} %get-tuple-element.28), channel_id=1, source_target_pairs={{0,16},{1,17},{2,18},{3,19},{4,20},{5,21},{6,22},{7,23},{8,24},{9,... | collective-permute-start | bytes 442376 | tf_op jit(solution)/shard_map/ppermute | solution.py:443
  85.3 1.9 %collective-permute-start.3 = (bf16[96,768]{1,0:T(8,128)(2,1)S(1)}, bf16[96,768]{1,0:T(8,128)(2,1)S(1)}, u32[]{:S(2)}, u32[]{:S(2)}) collective-permute-start(bf16[96,768]{1,0:T(8,128)(2,1)S(1)} %get-tuple-element.29), channel_id=1, source_target_pairs={{0,48},{1,49},{2,50},{3,51},{4,52},{5,53},{6,54},{7,55},{8,56},{9,... | collective-permute-start | bytes 442376 | tf_op jit(solution)/shard_map/ppermute | solution.py:443
  87.2 1.8 %collective-permute-start.2 = (bf16[96,768]{1,0:T(8,128)(2,1)S(1)}, bf16[96,768]{1,0:T(8,128)(2,1)S(1)}, u32[]{:S(2)}, u32[]{:S(2)}) collective-permute-start(bf16[96,768]{1,0:T(8,128)(2,1)S(1)} %get-tuple-element.30), channel_id=1, source_target_pairs={{0,32},{1,33},{2,34},{3,35},{4,36},{5,37},{6,38},{7,39},{8,40},{9,... | collective-permute-start | bytes 442376 | tf_op jit(solution)/shard_map/ppermute | solution.py:443
  89.0 2.1 %collective-permute-done.1 = bf16[96,768]{1,0:T(8,128)(2,1)S(1)} collective-permute-done((bf16[96,768]{1,0:T(8,128)(2,1)S(1)}, bf16[96,768]{1,0:T(8,128)(2,1)S(1)}, u32[]{:S(2)}, u32[]{:S(2)}) %collective-permute-start.1) | collective-permute-done | bytes 147488 | tf_op jit(solution)/shard_map/ppermute | solution.py:443
  91.1 2.5 %collective-permute-done.3 = bf16[96,768]{1,0:T(8,128)(2,1)S(1)} collective-permute-done((bf16[96,768]{1,0:T(8,128)(2,1)S(1)}, bf16[96,768]{1,0:T(8,128)(2,1)S(1)}, u32[]{:S(2)}, u32[]{:S(2)}) %collective-permute-start.3) | collective-permute-done | bytes 147488 | tf_op jit(solution)/shard_map/ppermute | solution.py:443
  93.5 1.7 %collective-permute-done.2 = bf16[96,768]{1,0:T(8,128)(2,1)S(1)} collective-permute-done((bf16[96,768]{1,0:T(8,128)(2,1)S(1)}, bf16[96,768]{1,0:T(8,128)(2,1)S(1)}, u32[]{:S(2)}, u32[]{:S(2)}) %collective-permute-start.2) | collective-permute-done | bytes 147488 | tf_op jit(solution)/shard_map/ppermute | solution.py:443
  95.2 0.1 add_convert_fusion.1
  95.4 16.4 %all_to_all.15 = bf16[8,12,768]{2,1,0:T(8,128)(2,1)S(1)} all-to-all(bf16[8,12,768]{2,1,0:T(8,128)(2,1)S(1)} %reshape.7), channel_id=1, replica_groups={{0,2,4,6,8,10,12,14},{1,3,5,7,9,11,13,15},{16,18,20,22,24,26,28,30},{17..., dimensions={0} | all-to-all | bytes 294912 | tf_op jit(solution)/shard_map/all_to_all | solution.py:457
  111.8 0.6 collective-permute-start.6
  112.4 2.4 %collective-permute-start.5 = (f32[12,768]{1,0:T(8,128)S(1)}, f32[12,768]{1,0:T(8,128)S(1)}, u32[]{:S(2)}, u32[]{:S(2)}) collective-permute-start(f32[12,768]{1,0:T(8,128)S(1)} %convert_reduce_fusion), channel_id=1, source_target_pairs={{0,128},{64,192},{128,0},{192,64},{1,129},{65,193},{129,1},{193,65... | collective-permute-start | bytes 110600 | tf_op jit(solution)/shard_map/ppermute | solution.py:447
  114.8 1.2 collective-permute-start.4
  116.0 4.9 %branch.1 = bf16[1024,768]{1,0:T(8,128)(2,1)} custom-call(bf16[1024,768]{1,0:T(8,128)(2,1)} %get-tuple-element.26.attn_ref, bf16[768,768]{1,0:T(8,128)(2,1)} %wout_ref.1), custom_call_target="tpu_custom_call" | custom-call | flops 1300000000 | bytes 5242880 | tf_op jit(solution)/shard_map/branch/pallas_call | solution.py:418
  120.9 0.0 collective-permute-done.6
  120.9 0.0 collective-permute-done.5
  120.9 0.0 collective-permute-done.4
  120.9 0.6 add_bitcast_fusion
  (4 shorter events, 0.1 us)
Async XLA Ops:
  8.6 12.8 %copy-start = (s32[16]{0:T(128)S(1)}, s32[16]{0:T(128)}, u32[]{:S(2)}) copy-start(s32[16]{0:T(128)} %off_ref.9) | copy-start | bytes 196
  8.7 40.3 %all-to-all-start = ((bf16[64,64,128]{2,1,0:T(8,128)(2,1)}), bf16[64,64,128]{2,1,0:T(8,128)(2,1)S(1)}, u32[]{:S(2)}, u32[]{:S(2)}) async-start(bf16[64,64,128]{2,1,0:T(8,128)(2,1)} %get-tuple-element.17), calls=%async_computation | async-start | bytes 2097152 | tf_op jit(solution)/shard_map/all_to_all | solution.py:469
  56.6 19.2 %all-to-all-start.1 = ((bf16[64,8,128]{2,1,0:T(8,128)(2,1)}), bf16[64,8,128]{2,1,0:T(8,128)(2,1)S(1)}, u32[]{:S(2)}, u32[]{:S(2)}) async-start(bf16[64,8,128]{2,1,0:T(8,128)(2,1)} %get-tuple-element.24), calls=%async_computation.1 | async-start | bytes 262144 | tf_op jit(solution)/shard_map/all_to_all | solution.py:472
  81.6 2.1 %collective-permute-start = (bf16[384,768]{1,0:T(8,128)(2,1)S(1)}, bf16[384,768]{1,0:T(8,128)(2,1)S(1)}, u32[]{:S(2)}, u32[]{:S(2)}) collective-permute-start(bf16[384,768]{1,0:T(8,128)(2,1)S(1)} %slice.19), channel_id=1, source_target_pairs={{0,1},{1,0},{2,3},{3,2},{4,5},{5,4},{6,7},{7,6},{8,9},{9,8},{10,11... | collective-permute-start | bytes 1769480 | tf_op jit(solution)/shard_map/ppermute | solution.py:439
  83.9 7.2 %collective-permute-start.1 = (bf16[96,768]{1,0:T(8,128)(2,1)S(1)}, bf16[96,768]{1,0:T(8,128)(2,1)S(1)}, u32[]{:S(2)}, u32[]{:S(2)}) collective-permute-start(bf16[96,768]{1,0:T(8,128)(2,1)S(1)} %get-tuple-element.28), channel_id=1, source_target_pairs={{0,16},{1,17},{2,18},{3,19},{4,20},{5,21},{6,22},{7,23},{8,24},{9,... | collective-permute-start | bytes 442376 | tf_op jit(solution)/shard_map/ppermute | solution.py:443
  85.3 8.2 %collective-permute-start.3 = (bf16[96,768]{1,0:T(8,128)(2,1)S(1)}, bf16[96,768]{1,0:T(8,128)(2,1)S(1)}, u32[]{:S(2)}, u32[]{:S(2)}) collective-permute-start(bf16[96,768]{1,0:T(8,128)(2,1)S(1)} %get-tuple-element.29), channel_id=1, source_target_pairs={{0,48},{1,49},{2,50},{3,51},{4,52},{5,53},{6,54},{7,55},{8,56},{9,... | collective-permute-start | bytes 442376 | tf_op jit(solution)/shard_map/ppermute | solution.py:443
  87.2 8.0 %collective-permute-start.2 = (bf16[96,768]{1,0:T(8,128)(2,1)S(1)}, bf16[96,768]{1,0:T(8,128)(2,1)S(1)}, u32[]{:S(2)}, u32[]{:S(2)}) collective-permute-start(bf16[96,768]{1,0:T(8,128)(2,1)S(1)} %get-tuple-element.30), channel_id=1, source_target_pairs={{0,32},{1,33},{2,34},{3,35},{4,36},{5,37},{6,38},{7,39},{8,40},{9,... | collective-permute-start | bytes 442376 | tf_op jit(solution)/shard_map/ppermute | solution.py:443
  111.8 9.1 %collective-permute-start.6 = (f32[12,768]{1,0:T(8,128)S(1)}, f32[12,768]{1,0:T(8,128)S(1)}, u32[]{:S(2)}, u32[]{:S(2)}) collective-permute-start(f32[12,768]{1,0:T(8,128)S(1)} %convert_reduce_fusion), channel_id=1, source_target_pairs={{0,192},{64,128},{128,64},{192,0},{1,193},{65,129},{129,65},{193,1... | collective-permute-start | bytes 110600 | tf_op jit(solution)/shard_map/ppermute | solution.py:447
  112.4 8.5 %collective-permute-start.5 = (f32[12,768]{1,0:T(8,128)S(1)}, f32[12,768]{1,0:T(8,128)S(1)}, u32[]{:S(2)}, u32[]{:S(2)}) collective-permute-start(f32[12,768]{1,0:T(8,128)S(1)} %convert_reduce_fusion), channel_id=1, source_target_pairs={{0,128},{64,192},{128,0},{192,64},{1,129},{65,193},{129,1},{193,65... | collective-permute-start | bytes 110600 | tf_op jit(solution)/shard_map/ppermute | solution.py:447
  114.8 6.1 %collective-permute-start.4 = (f32[12,768]{1,0:T(8,128)S(1)}, f32[12,768]{1,0:T(8,128)S(1)}, u32[]{:S(2)}, u32[]{:S(2)}) collective-permute-start(f32[12,768]{1,0:T(8,128)S(1)} %convert_reduce_fusion), channel_id=1, source_target_pairs={{0,64},{64,0},{128,192},{192,128},{1,65},{65,1},{129,193},{193,129... | collective-permute-start | bytes 110600 | tf_op jit(solution)/shard_map/ppermute | solution.py:447
where the time goes:
time: 122 us
  Pallas kernels  62.4 us (51%)
  starting transfers between devices  30.2 us (25%)
  blocking collectives  16.4 us (13%)
  waiting for transfers between devices  10.1 us (8%)
  between operations  1.42 us (1%)
    pallas_call x2, Pallas kernels, local(): pl.pallas_call(functools.partial(local_kernel, first, groups), grid=(grou...  36 us
    all_to_all x1, blocking collectives, reduce_gradient(): lax.all_to_all(blocks, 'seq', 0, 0, tiled=True, axis_index_groups=Z_GROUPS)  16.4 us
    all_to_all x1, starting transfers between devices, body(): recv = lax.all_to_all(send, 'seq', 0, 0, tiled=True)  12.1 us
    all_to_all x1, starting transfers between devices, body(): back = lax.all_to_all(ret, 'seq', 0, 0, tiled=True)  8.72 us
    pallas_call x1, Pallas kernels, pick(): pl.pallas_call(pick_kernel, in_specs=[SMEM, HBM, HBM, HBM, HBM], out_shap...  8.01 us
    pallas_call x1, Pallas kernels, far(): pl.pallas_call(far_kernel, in_specs=[SMEM, SMEM, SMEM, VMEM], out_specs=[...  7.65 us
    ppermute x3, waiting for transfers between devices, along_y(): lax.ppermute(a, 'seq', [(place(y, z, c), place((y + k) % 4, z, c)) for y,...  6.27 us
    pallas_call x1, Pallas kernels, merge(): pl.pallas_call(functools.partial(merge_kernel, split), in_specs=[SMEM] *...  5.81 us
  transfers between devices with their start and end apart: 9, of which 5 were waited for; matrix products, arithmetic and copies ran while one was open for 0% of the time, Pallas kernels for 34%

commit v1 on v0

--- a/solution.py
+++ b/solution.py
@@ -56,7 +56,7 @@
 VMEM = pl.BlockSpec(memory_space=pltpu.VMEM)
 
 
-def pick_kernel(off_ref, x_hbm, wq_hbm, wk_hbm, wv_hbm, send_ref, x_ref, w_ref, x2_ref, sems):
+def pick_kernel(off_ref, x_hbm, wq_hbm, wk_hbm, wv_hbm, send_hbm, x_ref, w_ref, x2_ref, send_ref, sems):
     copies = []
     for b in range(4):
         r = pl.ds(256 * b, 256)
@@ -90,6 +90,7 @@
         sel.append(jnp.concatenate(parts, axis=1))
     q, k, v = sel
     lane = lanes((64, 128))
+    stores = []
     for h in range(HEADS):
         t = min(48 * h // 128, 4)
         o = 48 * h - 128 * t
@@ -104,6 +105,11 @@
             s = slice(16 * j, 16 * j + 16)
             mine = jnp.concatenate([q_low[s], q_high[s], q_low[0:32]], axis=0)
             send_ref[4 * h + j] = jnp.where(lane < 96, kv, mine).astype(bf16)
+        part = pl.ds(4 * h, 4)
+        stores.append(pltpu.make_async_copy(send_ref.at[part], send_hbm.at[part], sems.at[13 + h]))
+        stores[h].start()
+    for store in stores:
+        store.wait()
 
 
 def pick(offsets, x, wq, wk, wv):
@@ -111,14 +117,15 @@
         pick_kernel,
         in_specs=[SMEM, HBM, HBM, HBM, HBM],
         out_shape=[
-            jax.ShapeDtypeStruct((SHARDS, PICKED, 128), bf16),
+            pltpu.HBM((SHARDS, PICKED, 128), bf16),
             pltpu.VMEM((SEG, D), bf16),
         ],
-        out_specs=[VMEM, VMEM],
+        out_specs=[HBM, VMEM],
         scratch_shapes=[
             pltpu.VMEM((3, D, D), bf16),
             pltpu.VMEM((SEG, D), bf16),
-            pltpu.SemaphoreType.DMA((13,)),
+            pltpu.VMEM((SHARDS, PICKED, 128), bf16),
+            pltpu.SemaphoreType.DMA((29,)),
         ],
         compiler_params=pltpu.CompilerParams(vmem_limit_bytes=24 << 20),
         name="pick",
@@ -242,6 +249,9 @@
         pltpu.VMEM((2 * groups, PICKED, 128), f32),
     ]
     scratch = [pltpu.VMEM((3, D, D), bf16), pltpu.VMEM((2, SEG, 128), f32), pltpu.VMEM((2, SEG, 128), f32)]
+    if first:
+        out_specs[0] = VMEM
+        out_shape[0] = pltpu.VMEM((2 * groups, SEG, 128), bf16)
     operands = (rank, count, offsets, vmem(x), *(hbm(w) for w in weights))
     in_specs = [SMEM, SMEM, SMEM, VMEM, HBM, HBM, HBM]
     if first == 0:
@@ -328,16 +338,13 @@
     return jnp.concatenate(out, axis=1)
 
 
-def merge_kernel(split, rank_ref, count_ref, off_ref, attn0_hbm, attn1_hbm, so0_ref, so1_ref, sl0_ref, sl1_ref, ret_ref, cot_hbm, attn_hbm, grad_ref, near_s, cot_s, attn_s, sems):
+def merge_kernel(split, rank_ref, count_ref, off_ref, attn0_hbm, attn1_ref, so0_ref, so1_ref, sl0_ref, sl1_ref, ret_ref, cot_hbm, attn_hbm, grad_ref, near_s, cot_s, attn_s, sems):
     loads = []
     for b in range(4):
         part = pl.ds(256 * b, 256)
-        loads.append([
-            pltpu.make_async_copy(attn0_hbm.at[:, part], near_s.at[0:split, part], sems.at[6 + 2 * b]),
-            pltpu.make_async_copy(attn1_hbm.at[:, part], near_s.at[split:PAIRS, part], sems.at[7 + 2 * b]),
-        ])
+        loads.append(pltpu.make_async_copy(attn0_hbm.at[:, part], near_s.at[:, part], sems.at[6 + b]))
     last_load = pltpu.make_async_copy(cot_hbm, cot_s, sems.at[5])
-    for copy in (*loads[0], *loads[1], *loads[2], *loads[3], last_load):
+    for copy in (*loads, last_load):
         copy.start()
     either = lambda early, late, p: early.at[p] if p < split else late.at[p - split]
     lane = lanes((PICKED, 128))
@@ -368,9 +375,8 @@
         r = slice(256 * b, 256 * b + 256)
         spread = (rows((256, PICKED)) // RATE + 16 * b == lanes((256, PICKED))).astype(bf16)
         far_rows = nn(spread, sel)
-        for copy in loads[b]:
-            copy.wait()
-        near_rows = natural(lambda p: near_s[p, r, :].astype(f32), 256)
+        loads[b].wait()
+        near_rows = natural(lambda p: either(near_s, attn1_ref, p)[r, :].astype(f32), 256)
         row = rows((256, D))
         attn = jnp.where(row % RATE == offcol, far_rows, near_rows)
         attn = jnp.where(row + (rank_ref[0] * SEG + 256 * b) < count_ref[0], attn, 0.0).astype(bf16)
@@ -394,11 +400,11 @@
     split = near0[0].shape[0]
     return pl.pallas_call(
         functools.partial(merge_kernel, split),
-        in_specs=[SMEM] * 3 + [HBM] * 2 + [VMEM] * 5 + [HBM],
+        in_specs=[SMEM] * 3 + [HBM] + [VMEM] * 6 + [HBM],
         out_specs=[HBM, VMEM],
         out_shape=[pltpu.HBM((SEG, D), bf16), jax.ShapeDtypeStruct((D, D), bf16)],
         scratch_shapes=[
-            pltpu.VMEM((PAIRS, SEG, 128), bf16),
+            pltpu.VMEM((split, SEG, 128), bf16),
             pltpu.VMEM((D, SEG), bf16),
             pltpu.VMEM((SEG, D), bf16),
             pltpu.SemaphoreType.DMA((14,)),
@@ -406,7 +412,7 @@
         compiler_params=pltpu.CompilerParams(vmem_limit_bytes=20 << 20),
         cost_estimate=pl.CostEstimate(flops=4_000_000_000, transcendentals=0, bytes_accessed=8 << 20),
         name="merge",
-    )(rank, count, offsets, hbm(near0[0]), hbm(near1[0]), *(vmem(a) for n in (1, 2) for a in (near0[n], near1[n])), vmem(ret), hbm(cot))
+    )(rank, count, offsets, hbm(near0[0]), vmem(near1[0]), *(vmem(a) for n in (1, 2) for a in (near0[n], near1[n])), vmem(ret), hbm(cot))
 
 
 def branch_kernel(attn_ref, wout_ref, branch_ref):

time: 122 us -> 121 us (level)
  transfers between devices with their start and end apart: 9 -> 9, of which waited for: 5 -> 6; matrix products, arithmetic and copies ran while one was open for 0% -> 0% of each run, Pallas kernels for 34% -> 33%
where the time goes in v1:
time: 121 us
  Pallas kernels  61.6 us (51%)
  starting transfers between devices  29.9 us (25%)
  blocking collectives  16.4 us (14%)
  waiting for transfers between devices  10.4 us (9%)
  between operations  1.4 us (1%)
    pallas_call x2, Pallas kernels, local(): pl.pallas_call(functools.partial(local_kernel, first, groups), grid=(grou...  35.3 us
    all_to_all x1, blocking collectives, reduce_gradient(): lax.all_to_all(blocks, 'seq', 0, 0, tiled=True, axis_index_groups=Z_GROUPS)  16.4 us
    all_to_all x1, starting transfers between devices, body(): recv = lax.all_to_all(send, 'seq', 0, 0, tiled=True)  12.1 us
    all_to_all x1, starting transfers between devices, body(): back = lax.all_to_all(ret, 'seq', 0, 0, tiled=True)  8.73 us
    pallas_call x1, Pallas kernels, pick(): pl.pallas_call(pick_kernel, in_specs=[SMEM, HBM, HBM, HBM, HBM], out_shap...  7.9 us
    pallas_call x1, Pallas kernels, far(): pl.pallas_call(far_kernel, in_specs=[SMEM, SMEM, SMEM, VMEM], out_specs=[...  7.74 us
    ppermute x3, waiting for transfers between devices, along_y(): lax.ppermute(a, 'seq', [(place(y, z, c), place((y + k) % 4, z, c)) for y,...  6.29 us
    pallas_call x1, Pallas kernels, merge(): pl.pallas_call(functools.partial(merge_kernel, split), in_specs=[SMEM] *...  5.76 us
  transfers between devices with their start and end apart: 9, of which 6 were waited for; matrix products, arithmetic and copies ran while one was open for 0% of the time, Pallas kernels for 33%

profile of v1, /device:TPU:6, one launch (start us, length us, event | category | flops | bytes accessed | tf_op | source)
XLA Modules:
  0.0 120.8 jit_solution(13397068951946903359)
XLA Ops:
  0.6 7.9 %pick.1 = (bf16[64,64,128]{2,1,0:T(8,128)(2,1)}, bf16[1024,768]{1,0:T(8,128)(2,1)S(1)}) custom-call(s32[16]{0:T(128)} %off_ref.9, bf16[1024,768]{1,0:T(8,128)(2,1)} %bitcast.6, bf16[768,768]{1,0:T(8,128)(2,1)} %wq_hbm.5, bf16[768,768]{1,0:T(8,128)(2,1)} %wk_hbm.5, bf16[768,768]{1,0:T(8,128)(2,1)} %wv_hbm.5), custom_call_target="tpu_custom_call" | custom-call | tf_op jit(solution)/shard_map/pick/pallas_call | solution.py:116
  8.5 0.0 copy-start
  8.5 12.1 %all-to-all-start = ((bf16[64,64,128]{2,1,0:T(8,128)(2,1)}), bf16[64,64,128]{2,1,0:T(8,128)(2,1)S(1)}, u32[]{:S(2)}, u32[]{:S(2)}) async-start(bf16[64,64,128]{2,1,0:T(8,128)(2,1)} %get-tuple-element.17), calls=%async_computation | async-start | bytes 2097152 | tf_op jit(solution)/shard_map/all_to_all | solution.py:475
  21.3 0.0 copy-done
  21.3 25.6 %local.2 = (bf16[6,1024,128]{2,1,0:T(8,128)(2,1)}, f32[6,64,128]{2,1,0:T(8,128)S(1)}, f32[6,64,128]{2,1,0:T(8,128)S(1)}, bf16[768,1024]{1,0:T(8,128)(2,1)}) custom-call(s32[1]{0:T(128)} %bitcast.rank_ref, s32[1]{0:T(128)S(6)} %copy.10.count_ref, s32[16]{0:T(128)S(1)} %copy-done, bf16[1024,768]{1,0:T(8,128)(2,1)S(1)} %get-tuple-element.15.x_ref, ...), custom_call_target="tpu_custom_call" | custom-call | flops 17999998976 | bytes 8388608 | tf_op jit(solution)/shard_map/local/pallas_call | solution.py:264
  47.0 1.8 %all-to-all-done.recv_ref = bf16[64,64,128]{2,1,0:T(8,128)(2,1)S(1)} async-done(((bf16[64,64,128]{2,1,0:T(8,128)(2,1)}), bf16[64,64,128]{2,1,0:T(8,128)(2,1)S(1)}, u32[]{:S(2)}, u32[]{:S(2)}) %all-to-all-start) | async-done | bytes 1048608 | tf_op jit(solution)/shard_map/all_to_all | solution.py:475
  48.8 7.7 %far.1 = (bf16[64,8,128]{2,1,0:T(8,128)(2,1)}, s32[1]{0:T(128)}) custom-call(s32[1]{0:T(128)} %bitcast.rank_ref, s32[1]{0:T(128)S(6)} %copy.10.count_ref, s32[16]{0:T(128)S(1)} %copy-done, bf16[64,64,128]{2,1,0:T(8,128)(2,1)S(1)} %all-to-all-done.recv_ref), custom_call_target="tpu_custom_call" | custom-call | flops 6000000000 | bytes 2097152 | tf_op jit(solution)/shard_map/far/pallas_call | solution.py:312
  56.6 8.7 %all-to-all-start.1 = ((bf16[64,8,128]{2,1,0:T(8,128)(2,1)}), bf16[64,8,128]{2,1,0:T(8,128)(2,1)S(1)}, u32[]{:S(2)}, u32[]{:S(2)}) async-start(bf16[64,8,128]{2,1,0:T(8,128)(2,1)} %get-tuple-element.24), calls=%async_computation.1 | async-start | bytes 262144 | tf_op jit(solution)/shard_map/all_to_all | solution.py:478
  65.3 9.7 %local.3 = (bf16[2,1024,128]{2,1,0:T(8,128)(2,1)S(1)}, f32[2,64,128]{2,1,0:T(8,128)S(1)}, f32[2,64,128]{2,1,0:T(8,128)S(1)}) custom-call(s32[1]{0:T(128)} %bitcast.rank_ref, s32[1]{0:T(128)} %get-tuple-element.18.count_ref, s32[16]{0:T(128)S(1)} %copy-done, bf16[1024,768]{1,0:T(8,128)(2,1)S(1)} %get-tuple-element.15.x_ref, bf16[768,768]{1,0:T(8,128)(2,1)} %wq_hbm.5, ...), custom_call_target="tpu_custom_call" | custom-call | flops 6000000000 | bytes 8388608 | tf_op jit(solution)/shard_map/local/pallas_call | solution.py:264
  75.0 0.4 all-to-all-done.1.ret_ref
  75.4 5.8 %merge.1 = (bf16[1024,768]{1,0:T(8,128)(2,1)}, bf16[768,768]{1,0:T(8,128)(2,1)S(1)}) custom-call(s32[1]{0:T(128)} %bitcast.rank_ref, s32[1]{0:T(128)S(6)} %copy.10.count_ref, s32[16]{0:T(128)S(1)} %copy-done, bf16[6,1024,128]{2,1,0:T(8,128)(2,1)} %get-tuple-element.16.attn0_hbm, bf16[2,1024,128]{2,1,0:T(8,128)(2,1)S(1)} %get-tuple-element.19.attn1_ref, ...), custom_call_target="tpu_custom_call" | custom-call | flops 4000000000 | bytes 8388608 | tf_op jit(solution)/shard_map/merge/pallas_call | solution.py:401
  81.2 0.2 collective-permute-start
  81.4 1.9 %collective-permute-done = bf16[384,768]{1,0:T(8,128)(2,1)S(1)} collective-permute-done((bf16[384,768]{1,0:T(8,128)(2,1)S(1)}, bf16[384,768]{1,0:T(8,128)(2,1)S(1)}, u32[]{:S(2)}, u32[]{:S(2)}) %collective-permute-start) | collective-permute-done | bytes 589856 | tf_op jit(solution)/shard_map/ppermute | solution.py:445
  83.3 0.2 add_convert_fusion
  83.5 1.1 collective-permute-start.1
  84.6 2.2 %collective-permute-start.3 = (bf16[96,768]{1,0:T(8,128)(2,1)S(1)}, bf16[96,768]{1,0:T(8,128)(2,1)S(1)}, u32[]{:S(2)}, u32[]{:S(2)}) collective-permute-start(bf16[96,768]{1,0:T(8,128)(2,1)S(1)} %get-tuple-element.29), channel_id=1, source_target_pairs={{0,48},{1,49},{2,50},{3,51},{4,52},{5,53},{6,54},{7,55},{8,56},{9,... | collective-permute-start | bytes 442376 | tf_op jit(solution)/shard_map/ppermute | solution.py:449
  86.8 1.4 %collective-permute-start.2 = (bf16[96,768]{1,0:T(8,128)(2,1)S(1)}, bf16[96,768]{1,0:T(8,128)(2,1)S(1)}, u32[]{:S(2)}, u32[]{:S(2)}) collective-permute-start(bf16[96,768]{1,0:T(8,128)(2,1)S(1)} %get-tuple-element.30), channel_id=1, source_target_pairs={{0,32},{1,33},{2,34},{3,35},{4,36},{5,37},{6,38},{7,39},{8,40},{9,... | collective-permute-start | bytes 442376 | tf_op jit(solution)/shard_map/ppermute | solution.py:449
  88.2 2.6 %collective-permute-done.1 = bf16[96,768]{1,0:T(8,128)(2,1)S(1)} collective-permute-done((bf16[96,768]{1,0:T(8,128)(2,1)S(1)}, bf16[96,768]{1,0:T(8,128)(2,1)S(1)}, u32[]{:S(2)}, u32[]{:S(2)}) %collective-permute-start.1) | collective-permute-done | bytes 147488 | tf_op jit(solution)/shard_map/ppermute | solution.py:449
  90.8 2.3 %collective-permute-done.3 = bf16[96,768]{1,0:T(8,128)(2,1)S(1)} collective-permute-done((bf16[96,768]{1,0:T(8,128)(2,1)S(1)}, bf16[96,768]{1,0:T(8,128)(2,1)S(1)}, u32[]{:S(2)}, u32[]{:S(2)}) %collective-permute-start.3) | collective-permute-done | bytes 147488 | tf_op jit(solution)/shard_map/ppermute | solution.py:449
  93.1 1.4 %collective-permute-done.2 = bf16[96,768]{1,0:T(8,128)(2,1)S(1)} collective-permute-done((bf16[96,768]{1,0:T(8,128)(2,1)S(1)}, bf16[96,768]{1,0:T(8,128)(2,1)S(1)}, u32[]{:S(2)}, u32[]{:S(2)}) %collective-permute-start.2) | collective-permute-done | bytes 147488 | tf_op jit(solution)/shard_map/ppermute | solution.py:449
  94.5 0.1 add_convert_fusion.1
  94.6 16.4 %all_to_all.15 = bf16[8,12,768]{2,1,0:T(8,128)(2,1)S(1)} all-to-all(bf16[8,12,768]{2,1,0:T(8,128)(2,1)S(1)} %reshape.7), channel_id=1, replica_groups={{0,2,4,6,8,10,12,14},{1,3,5,7,9,11,13,15},{16,18,20,22,24,26,28,30},{17..., dimensions={0} | all-to-all | bytes 294912 | tf_op jit(solution)/shard_map/all_to_all | solution.py:463
  111.0 0.6 collective-permute-start.6
  111.6 2.4 %collective-permute-start.5 = (f32[12,768]{1,0:T(8,128)S(1)}, f32[12,768]{1,0:T(8,128)S(1)}, u32[]{:S(2)}, u32[]{:S(2)}) collective-permute-start(f32[12,768]{1,0:T(8,128)S(1)} %convert_reduce_fusion), channel_id=1, source_target_pairs={{0,128},{64,192},{128,0},{192,64},{1,129},{65,193},{129,1},{193,65... | collective-permute-start | bytes 110600 | tf_op jit(solution)/shard_map/ppermute | solution.py:453
  114.0 1.2 collective-permute-start.4
  115.2 4.9 %branch.1 = bf16[1024,768]{1,0:T(8,128)(2,1)} custom-call(bf16[1024,768]{1,0:T(8,128)(2,1)} %get-tuple-element.26.attn_ref, bf16[768,768]{1,0:T(8,128)(2,1)} %wout_ref.1), custom_call_target="tpu_custom_call" | custom-call | flops 1300000000 | bytes 5242880 | tf_op jit(solution)/shard_map/branch/pallas_call | solution.py:424
  120.1 0.0 collective-permute-done.6
  120.1 0.0 collective-permute-done.5
  120.1 0.0 collective-permute-done.4
  120.1 0.6 add_bitcast_fusion
  (4 shorter events, 0.1 us)
Async XLA Ops:
  8.5 12.8 %copy-start = (s32[16]{0:T(128)S(1)}, s32[16]{0:T(128)}, u32[]{:S(2)}) copy-start(s32[16]{0:T(128)} %off_ref.9) | copy-start | bytes 196
  8.5 40.3 %all-to-all-start = ((bf16[64,64,128]{2,1,0:T(8,128)(2,1)}), bf16[64,64,128]{2,1,0:T(8,128)(2,1)S(1)}, u32[]{:S(2)}, u32[]{:S(2)}) async-start(bf16[64,64,128]{2,1,0:T(8,128)(2,1)} %get-tuple-element.17), calls=%async_computation | async-start | bytes 2097152 | tf_op jit(solution)/shard_map/all_to_all | solution.py:475
  56.6 18.8 %all-to-all-start.1 = ((bf16[64,8,128]{2,1,0:T(8,128)(2,1)}), bf16[64,8,128]{2,1,0:T(8,128)(2,1)S(1)}, u32[]{:S(2)}, u32[]{:S(2)}) async-start(bf16[64,8,128]{2,1,0:T(8,128)(2,1)} %get-tuple-element.24), calls=%async_computation.1 | async-start | bytes 262144 | tf_op jit(solution)/shard_map/all_to_all | solution.py:478
  81.2 2.1 %collective-permute-start = (bf16[384,768]{1,0:T(8,128)(2,1)S(1)}, bf16[384,768]{1,0:T(8,128)(2,1)S(1)}, u32[]{:S(2)}, u32[]{:S(2)}) collective-permute-start(bf16[384,768]{1,0:T(8,128)(2,1)S(1)} %slice.19), channel_id=1, source_target_pairs={{0,1},{1,0},{2,3},{3,2},{4,5},{5,4},{6,7},{7,6},{8,9},{9,8},{10,11... | collective-permute-start | bytes 1769480 | tf_op jit(solution)/shard_map/ppermute | solution.py:445
  83.5 7.4 %collective-permute-start.1 = (bf16[96,768]{1,0:T(8,128)(2,1)S(1)}, bf16[96,768]{1,0:T(8,128)(2,1)S(1)}, u32[]{:S(2)}, u32[]{:S(2)}) collective-permute-start(bf16[96,768]{1,0:T(8,128)(2,1)S(1)} %get-tuple-element.28), channel_id=1, source_target_pairs={{0,16},{1,17},{2,18},{3,19},{4,20},{5,21},{6,22},{7,23},{8,24},{9,... | collective-permute-start | bytes 442376 | tf_op jit(solution)/shard_map/ppermute | solution.py:449
  84.6 8.6 %collective-permute-start.3 = (bf16[96,768]{1,0:T(8,128)(2,1)S(1)}, bf16[96,768]{1,0:T(8,128)(2,1)S(1)}, u32[]{:S(2)}, u32[]{:S(2)}) collective-permute-start(bf16[96,768]{1,0:T(8,128)(2,1)S(1)} %get-tuple-element.29), channel_id=1, source_target_pairs={{0,48},{1,49},{2,50},{3,51},{4,52},{5,53},{6,54},{7,55},{8,56},{9,... | collective-permute-start | bytes 442376 | tf_op jit(solution)/shard_map/ppermute | solution.py:449
  86.8 7.7 %collective-permute-start.2 = (bf16[96,768]{1,0:T(8,128)(2,1)S(1)}, bf16[96,768]{1,0:T(8,128)(2,1)S(1)}, u32[]{:S(2)}, u32[]{:S(2)}) collective-permute-start(bf16[96,768]{1,0:T(8,128)(2,1)S(1)} %get-tuple-element.30), channel_id=1, source_target_pairs={{0,32},{1,33},{2,34},{3,35},{4,36},{5,37},{6,38},{7,39},{8,40},{9,... | collective-permute-start | bytes 442376 | tf_op jit(solution)/shard_map/ppermute | solution.py:449
  111.0 9.1 %collective-permute-start.6 = (f32[12,768]{1,0:T(8,128)S(1)}, f32[12,768]{1,0:T(8,128)S(1)}, u32[]{:S(2)}, u32[]{:S(2)}) collective-permute-start(f32[12,768]{1,0:T(8,128)S(1)} %convert_reduce_fusion), channel_id=1, source_target_pairs={{0,192},{64,128},{128,64},{192,0},{1,193},{65,129},{129,65},{193,1... | collective-permute-start | bytes 110600 | tf_op jit(solution)/shard_map/ppermute | solution.py:453
  111.6 8.5 %collective-permute-start.5 = (f32[12,768]{1,0:T(8,128)S(1)}, f32[12,768]{1,0:T(8,128)S(1)}, u32[]{:S(2)}, u32[]{:S(2)}) collective-permute-start(f32[12,768]{1,0:T(8,128)S(1)} %convert_reduce_fusion), channel_id=1, source_target_pairs={{0,128},{64,192},{128,0},{192,64},{1,129},{65,193},{129,1},{193,65... | collective-permute-start | bytes 110600 | tf_op jit(solution)/shard_map/ppermute | solution.py:453
  114.0 6.1 %collective-permute-start.4 = (f32[12,768]{1,0:T(8,128)S(1)}, f32[12,768]{1,0:T(8,128)S(1)}, u32[]{:S(2)}, u32[]{:S(2)}) collective-permute-start(f32[12,768]{1,0:T(8,128)S(1)} %convert_reduce_fusion), channel_id=1, source_target_pairs={{0,64},{64,0},{128,192},{192,128},{1,65},{65,1},{129,193},{193,129... | collective-permute-start | bytes 110600 | tf_op jit(solution)/shard_map/ppermute | solution.py:453
